TPU v7x, 32 devices: a whole 2x2x4 slice. The times are simulated.
32 devices in a mesh: gx: 4 (over y, x), gy: 2 (over core), gz: 4 (over z).
Axes of the slice: x: 2, y: 2, z: 4, core: 2. Of those that a mesh axis runs over, the one named last changes fastest.
Arguments:
- measures: float32 [65536, 256], P(('gx', 'gy', 'gz')), may hold values from -6 to 6
- group_index: int32 [65536], P(('gx', 'gy', 'gz')), may hold values from 0 to 511, as said below
- distinct_keys: int32 [32, 512], P(('gx', 'gy', 'gz')), may hold values from 32 to 65567, as said below
- group_counts: int32 [32], P(('gx', 'gy', 'gz')), may hold values from 128 to 512, as said below
Outputs:
- group_sums: float32 [16384, 256], P(('gx', 'gy', 'gz'))
- group_rows: int32 [16384], P(('gx', 'gy', 'gz'))
- group_keys: int32 [16384], P(('gx', 'gy', 'gz'))
- group_total: int32 [], replicated
Inputs may be any that keep to these rules, and one draw needn't show every extreme that they name: `group_counts`: every device has between 128 and 512 groups, and some device has exactly 512. `group_index`: each row's index lies below its device's group count, and every group of a device has at least one row. `distinct_keys`: each device's keys rise strictly; all keys of device d equal d modulo 32, so no key lives on two devices; entries at and past the device's count are unused.
All inputs are finite; a program needn't handle non-finite values.
Results may differ from a plain program's by a relative error of at most 0.0003.
Values sent between devices are 32-bit elements; how exact they have to be, the bound alone decides.
A program may use at most 64 MiB of HBM per device.

v0:
```python
import jax
import jax.numpy as jnp
from jax import lax
from jax.sharding import PartitionSpec as P


def shards(measures, group_index, distinct_keys, group_counts):
    rows, width = measures.shape
    span = distinct_keys.shape[1]
    devices = lax.axis_size(("gx", "gy", "gz"))
    slots = span // devices
    plane = lax.axis_size("gx") * lax.axis_size("gy")
    line = lax.axis_size("gz")
    count = group_counts[0]
    myself = jnp.int32(0)
    sender_counts = lax.all_gather(group_counts, ("gx", "gy", "gz"), axis=0, tiled=True)
    sender_offsets = jnp.cumsum(sender_counts) - sender_counts
    myself = lax.axis_index(("gx", "gy", "gz"))
    offset = sender_offsets[myself]
    group_total = jnp.sum(sender_counts)
    block = min(1024, rows)
    labels = lax.broadcasted_iota(jnp.int32, (span, block), 0)

    def accumulate(step, carry):
        totals, tallies = carry
        start = step * block
        index = lax.dynamic_slice_in_dim(group_index, start, block)
        values = lax.dynamic_slice_in_dim(measures, start, block, 0)
        hits = index[None, :] == labels
        totals = totals + jnp.dot(
            hits.astype(jnp.float32),
            values,
            precision=lax.Precision.HIGHEST,
            preferred_element_type=jnp.float32,
        )
        tallies = tallies + jnp.sum(hits, axis=1, dtype=jnp.int32)
        return (totals, tallies)

    sums, tallies = lax.fori_loop(
        0,
        rows // block,
        accumulate,
        (jnp.zeros((span, width), jnp.float32), jnp.zeros((span,), jnp.int32)),
    )
    local = jnp.arange(span, dtype=jnp.int32)
    live = local < count
    keys = jnp.where(live, distinct_keys[0], -1)
    fields = jnp.stack([tallies.astype(jnp.float32), keys.astype(jnp.float32)], axis=1)
    extra = fields.shape[1]

    def arrange(array):
        shaped = array.reshape((slots, devices) + array.shape[1:])
        rolled = jnp.roll(shaped, offset, axis=1)
        return rolled.reshape((slots, plane, line) + array.shape[1:])

    outgoing = (arrange(sums), arrange(fields))
    arrived = (
        lax.all_to_all(
            lax.all_to_all(outgoing[0], "gz", split_axis=2, concat_axis=2, tiled=True),
            ("gx", "gy"),
            split_axis=1,
            concat_axis=1,
            tiled=True,
        ),
        lax.all_to_all(
            lax.all_to_all(outgoing[1], "gz", split_axis=2, concat_axis=2, tiled=True),
            ("gx", "gy"),
            split_axis=1,
            concat_axis=1,
            tiled=True,
        ),
    )
    got_sums, got_fields = arrived
    got_fields = got_fields.reshape(-1, extra)
    sender = jnp.arange(devices, dtype=jnp.int32).reshape(1, plane, line)
    start_of = sender_offsets.reshape(1, plane, line)
    count_of = sender_counts.reshape(1, plane, line)
    level = jnp.arange(slots, dtype=jnp.int32).reshape(slots, 1, 1)
    position = level * devices + (myself - start_of) % devices
    arrived_live = (position < count_of) & (sender >= 0)
    target = jnp.where(arrived_live, (start_of + position) // devices, span).reshape(-1)
    group_sums = (
        jnp.zeros((span, width), jnp.float32)
        .at[target]
        .set(got_sums.reshape(-1, width), mode="drop")
    )
    group_rows = (
        jnp.zeros((span,), jnp.int32)
        .at[target]
        .set(got_fields[:, 0].astype(jnp.int32), mode="drop")
    )
    group_keys = (
        jnp.full((span,), -1, jnp.int32)
        .at[target]
        .set(got_fields[:, 1].astype(jnp.int32), mode="drop")
    )
    return (group_sums, group_rows, group_keys, group_total)


def solution(mesh):
    return jax.shard_map(
        shards,
        mesh=mesh,
        in_specs=(
            P(("gx", "gy", "gz"), None),
            P(("gx", "gy", "gz")),
            P(("gx", "gy", "gz"), None),
            P(("gx", "gy", "gz")),
        ),
        out_specs=(P(("gx", "gy", "gz"), None), P(("gx", "gy", "gz")), P(("gx", "gy", "gz")), P()),
        check_vma=False,
    )
```

profile of v0, /device:TPU:0, one launch (start us, length us, event | category | flops | bytes accessed | tf_op | source)
XLA Modules:
  0.0 106.3 jit_solution(15189355763401430567)
XLA Ops:
  1.3 0.1 dynamic-update-slice
  1.4 42.0 %all-reduce = s32[32]{0:T(128)S(1)} all-reduce(s32[32]{0:T(128)S(1)} %dynamic-update-slice), channel_id=1, replica_groups=mesh['gx'=4,'gy'=2,'gz'=4] {'gx','gy','gz'}, use_global_device_ids=true, to_apply=%add | all-reduce | flops 32 | bytes 256
  43.4 0.1 copy.37
  43.5 0.1 reduce.1
  43.6 0.6 fusion.19
  44.3 0.6 dynamic_slice.25
  46.8 7.4 %while.16 = (s32[]{:T(128)}, f32[512,256]{1,0:T(8,128)S(1)}, s32[512]{0:T(512)S(1)}, s32[2048]{0:T(1024)}, f32[2048,256]{1,0:T(8,128)}, /*index=5*/s32[]{:T(128)}, s32[]{:T(128)}, s32[]{:T(128)}, s32[]{:T(128)}) while((s32[]{:T(128)}, f32[512,256]{1,0:T(8,128)S(1)}, s32[512]{0:T(512)S(1)}, s32[2048]{0:T(1024)}, ...), condition=%wide.region_3.4_spmd.clone, body=%wide.region_1.3_spmd.clone.sunk | while | flops 1612972544 | bytes 2121886 | solution.py:39
  46.9 0.7 dynamic_slice.55
  47.6 2.7 %fusion.24 = f32[512,256]{1,0:T(8,128)S(1)} fusion(f32[2048,256]{1,0:T(8,128)} %get-tuple-element.203, s32[]{:T(128)S(6)} %select_n.107, s32[1024]{0:T(1024)S(1)} %dynamic_slice.55, f32[512,256]{1,0:T(8,128)S(1)} %get-tuple-element.191, pred[]{:T(512)S(6)} %compare.20), kind=kOutput, calls=%fused_computation.8.clone.1 | convolution fusion | flops 1611399168 | bytes 2101253 | tf_op jit(solution)/shard_map/while/body/eval_jaxpr/dot_general | solution.py:30
  50.2 0.3 fusion.25
  50.6 0.7 dynamic_slice.55
  51.2 2.7 %fusion.24 = f32[512,256]{1,0:T(8,128)S(1)} fusion(f32[2048,256]{1,0:T(8,128)} %get-tuple-element.203, s32[]{:T(128)S(6)} %select_n.107, s32[1024]{0:T(1024)S(1)} %dynamic_slice.55, f32[512,256]{1,0:T(8,128)S(1)} %get-tuple-element.191, pred[]{:T(512)S(6)} %compare.20), kind=kOutput, calls=%fused_computation.8.clone.1 | convolution fusion | flops 1611399168 | bytes 2101253 | tf_op jit(solution)/shard_map/while/body/eval_jaxpr/dot_general | solution.py:30
  53.9 0.3 fusion.25
  54.3 0.5 broadcast.199
  54.8 0.7 reduce.5
  55.5 0.1 squeeze.13
  55.6 0.1 fusion.13
  55.7 0.1 copy.42
  55.8 0.7 reshape.312
  56.5 3.6 %all-to-all-start.2 = ((f32[4,1,256]{2,1,0:T(1,128)}), f32[4,1,256]{2,1,0:T(1,128)S(1)}, u32[]{:S(2)}, u32[]{:S(2)}) async-start(f32[4,1,256]{2,1,0:T(1,128)} %reshape.312), calls=%async_computation.2 | async-start | bytes 8192 | tf_op jit(solution)/shard_map/all_to_all | solution.py:66
  60.1 0.1 fusion.9
  60.2 0.3 copy.38
  60.5 1.1 %copy.39 = f32[16,8,4,256]{3,1,0,2:T(8,128)} copy(f32[16,8,4,256]{3,0,2,1:T(8,128)S(1)} %bitcast.23) | data formatting | bytes 1048576 | tf_op jit(solution)/shard_map/reshape | solution.py:54
  61.6 4.0 %all-to-all-done.2 = f32[4,1,256]{2,1,0:T(1,128)S(1)} async-done(((f32[4,1,256]{2,1,0:T(1,128)}), f32[4,1,256]{2,1,0:T(1,128)S(1)}, u32[]{:S(2)}, u32[]{:S(2)}) %all-to-all-start.2) | async-done | bytes 4128 | tf_op jit(solution)/shard_map/all_to_all | solution.py:66
  65.6 3.5 %all-to-all-start = ((f32[16,8,4,256]{3,1,0,2:T(8,128)}), f32[16,8,4,256]{3,1,0,2:T(8,128)S(1)}, u32[]{:S(2)}, u32[]{:S(2)}) async-start(f32[16,8,4,256]{3,1,0,2:T(8,128)} %copy.39), calls=%async_computation | async-start | bytes 1048576 | tf_op jit(solution)/shard_map/all_to_all | solution.py:59
  69.1 0.1 reshape.258
  69.2 0.1 add_add_fusion
  69.3 0.5 broadcast.200
  69.8 0.7 reduce.6
  70.5 0.1 reshape.313
  70.6 0.7 reshape.314
  71.3 10.3 %all-to-all-done = f32[16,8,4,256]{3,1,0,2:T(8,128)S(1)} async-done(((f32[16,8,4,256]{3,1,0,2:T(8,128)}), f32[16,8,4,256]{3,1,0,2:T(8,128)S(1)}, u32[]{:S(2)}, u32[]{:S(2)}) %all-to-all-start) | async-done | bytes 524320 | tf_op jit(solution)/shard_map/all_to_all | solution.py:59
  81.6 3.6 %all-to-all-start.3 = ((f32[8,1,128]{2,1,0:T(1,128)}), f32[8,1,128]{2,1,0:T(1,128)S(1)}, u32[]{:S(2)}, u32[]{:S(2)}) async-start(f32[8,1,128]{2,1,0:T(1,128)} %reshape.314), calls=%async_computation.3 | async-start | bytes 8192 | tf_op jit(solution)/shard_map/all_to_all | solution.py:65
  85.2 1.1 %copy.40 = f32[16,8,4,256]{3,2,0,1:T(4,128)} copy(f32[16,8,4,256]{3,1,0,2:T(8,128)S(1)} %all-to-all-done) | data formatting | bytes 1048576 | tf_op jit(solution)/shard_map/all_to_all | solution.py:59
  86.4 3.5 %all-to-all-done.3 = f32[8,1,128]{2,1,0:T(1,128)S(1)} async-done(((f32[8,1,128]{2,1,0:T(1,128)}), f32[8,1,128]{2,1,0:T(1,128)S(1)}, u32[]{:S(2)}, u32[]{:S(2)}) %all-to-all-start.3) | async-done | bytes 4128 | tf_op jit(solution)/shard_map/all_to_all | solution.py:65
  89.8 3.5 %all-to-all-start.1 = ((f32[16,8,4,256]{3,2,0,1:T(4,128)}), f32[16,8,4,256]{3,2,0,1:T(4,128)S(1)}, u32[]{:S(2)}, u32[]{:S(2)}) async-start(f32[16,8,4,256]{3,2,0,1:T(4,128)} %copy.40), calls=%async_computation.1 | async-start | bytes 1048576 | tf_op jit(solution)/shard_map/all_to_all | solution.py:58
  93.3 0.1 fusion.12
  93.4 0.1 add.155
  93.5 0.1 and.67
  93.7 0.7 reduce.7
  94.4 0.1 reshape.315
  94.5 0.2 copy.45
  94.6 0.1 reshape.266
  94.8 3.0 %scatter_custom_fusion.1 = s32[512]{0:T(512)} fusion(s32[512]{0:T(512)S(1)} %bitcast.30, s32[512]{0:T(512)S(1)} %bitcast.34, s32[]{:T(128)} %constant.107.clone.1), kind=kCustom, calls=%fused_computation.40 | custom fusion | bytes 2052 | tf_op jit(solution)/shard_map/scatter | solution.py:90
  97.8 3.0 %scatter_custom_fusion.2 = s32[512]{0:T(512)} fusion(s32[512]{0:T(512)S(1)} %bitcast.31, s32[512]{0:T(512)S(1)} %bitcast.33, s32[]{:T(128)} %constant.111.clone.1), kind=kCustom, calls=%fused_computation.38 | custom fusion | bytes 2052 | tf_op jit(solution)/shard_map/scatter | solution.py:95
  100.8 2.2 %all-to-all-done.1 = f32[16,8,4,256]{3,2,0,1:T(4,128)S(1)} async-done(((f32[16,8,4,256]{3,2,0,1:T(4,128)}), f32[16,8,4,256]{3,2,0,1:T(4,128)S(1)}, u32[]{:S(2)}, u32[]{:S(2)}) %all-to-all-start.1) | async-done | bytes 524320 | tf_op jit(solution)/shard_map/all_to_all | solution.py:58
  103.0 0.2 reshape.271
  103.2 3.0 %scatter_custom_fusion = f32[512,256]{1,0:T(8,128)} fusion(s32[512]{0:T(512)S(1)} %bitcast.32, f32[512,256]{1,0:T(8,128)S(1)} %reshape.271, f32[]{:T(128)} %constant.100.clone.1), kind=kCustom, calls=%fused_computation.16 | custom fusion | bytes 524292 | tf_op jit(solution)/shard_map/scatter | solution.py:85
  (20 shorter events, 0.4 us)
Async XLA Ops:
  46.8 8.0 %copy-start = (s32[1,512]{1,0:T(1,128)S(1)}, s32[1,512]{1,0:T(1,128)}, u32[]{:S(2)}) copy-start(s32[1,512]{1,0:T(1,128)} %param.8) | copy-start | bytes 6148
  56.5 9.2 %all-to-all-start.2 = ((f32[4,1,256]{2,1,0:T(1,128)}), f32[4,1,256]{2,1,0:T(1,128)S(1)}, u32[]{:S(2)}, u32[]{:S(2)}) async-start(f32[4,1,256]{2,1,0:T(1,128)} %reshape.312), calls=%async_computation.2 | async-start | bytes 8192 | tf_op jit(solution)/shard_map/all_to_all | solution.py:66
  65.6 16.0 %all-to-all-start = ((f32[16,8,4,256]{3,1,0,2:T(8,128)}), f32[16,8,4,256]{3,1,0,2:T(8,128)S(1)}, u32[]{:S(2)}, u32[]{:S(2)}) async-start(f32[16,8,4,256]{3,1,0,2:T(8,128)} %copy.39), calls=%async_computation | async-start | bytes 1048576 | tf_op jit(solution)/shard_map/all_to_all | solution.py:59
  81.6 8.2 %all-to-all-start.3 = ((f32[8,1,128]{2,1,0:T(1,128)}), f32[8,1,128]{2,1,0:T(1,128)S(1)}, u32[]{:S(2)}, u32[]{:S(2)}) async-start(f32[8,1,128]{2,1,0:T(1,128)} %reshape.314), calls=%async_computation.3 | async-start | bytes 8192 | tf_op jit(solution)/shard_map/all_to_all | solution.py:65
  89.8 13.2 %all-to-all-start.1 = ((f32[16,8,4,256]{3,2,0,1:T(4,128)}), f32[16,8,4,256]{3,2,0,1:T(4,128)S(1)}, u32[]{:S(2)}, u32[]{:S(2)}) async-start(f32[16,8,4,256]{3,2,0,1:T(4,128)} %copy.40), calls=%async_computation.1 | async-start | bytes 1048576 | tf_op jit(solution)/shard_map/all_to_all | solution.py:58
where the time goes:
time: 107 us; the launch traced here: 106 us
  blocking collectives  42 us (39%)
  waiting for transfers between devices  20.1 us (19%)
  local copies, waits for them, and re-layouts  17.5 us (16%)
  starting transfers between devices  14.1 us (13%)
  matrix products  5.34 us (5%)
  other arithmetic  3.86 us (4%)
  between operations  3.41 us (3%)
    unnamed x1, blocking collectives  42 us
    all_to_all x1, waiting for transfers between devices, shards(): lax.all_to_all(outgoing[0], 'gz', split_axis=2, concat_axis=2, tiled=True)  10.3 us
    dot_general x2, matrix products, accumulate(): jnp.dot(hits.astype(jnp.float32), values, precision=lax.Precision.HIGHEST...  5.34 us
    all_to_all x1, waiting for transfers between devices, shards(): lax.all_to_all(outgoing[1], 'gz', split_axis=2, concat_axis=2, tiled=True)  4.02 us
    all_to_all x1, starting transfers between devices, shards(): lax.all_to_all(outgoing[1], 'gz', split_axis=2, concat_axis=2, tiled=True)  3.6 us
    all_to_all x1, starting transfers between devices, shards(): lax.all_to_all(lax.all_to_all(outgoing[1], 'gz', split_axis=2, concat_axi...  3.56 us
    all_to_all x1, starting transfers between devices, shards(): lax.all_to_all(lax.all_to_all(outgoing[0], 'gz', split_axis=2, concat_axi...  3.49 us
    all_to_all x1, starting transfers between devices, shards(): lax.all_to_all(outgoing[0], 'gz', split_axis=2, concat_axis=2, tiled=True)  3.47 us
  transfers between devices with their start and end apart: 4, of which 4 were waited for; matrix products, arithmetic and copies ran while one was open for 12% of the time, Pallas kernels for 0%

commit v1 on v0

v1 whole, which is shorter than its diff:
```python
import functools

import jax
import jax.numpy as jnp
from jax import lax
from jax.experimental import pallas as pl
from jax.experimental.pallas import tpu as pltpu
from jax.sharding import PartitionSpec as P

AXES = ("gx", "gy", "gz")
LANES = 128
MESH = pl.DeviceIdType.MESH


def round_up(value, unit):
    return (value + unit - 1) // unit * unit


def exchange_kernel(
    shape,
    index_ref,
    keys_ref,
    count_ref,
    measures_ref,
    recv_ref,
    counts_ref,
    held,
    stage,
    send,
    tally_ref,
    cbuf,
    load_sem,
    csend_sem,
    crecv_sem,
    send_sem,
    recv_sem,
):
    devices, ny, nz, span, levels, chunks, fields_at = shape
    me = (lax.axis_index("gx") * ny + lax.axis_index("gy")) * nz + lax.axis_index("gz")
    rows, width = held.shape
    chunk = rows // chunks
    halves = width // LANES
    sent_rows = fields_at + 2

    loads = []
    for c in range(chunks):
        piece = pl.ds(c * chunk, chunk)
        load = pltpu.make_async_copy(measures_ref.at[piece], held.at[piece], load_sem.at[c])
        load.start()
        loads.append(load)

    def place(k):
        other = lax.rem(me + k, devices)
        return other, (other // (ny * nz), lax.rem(other // nz, ny), lax.rem(other, nz))

    barrier = pltpu.get_barrier_semaphore()

    def greet(k, carry):
        _, spot = place(k)
        pl.semaphore_signal(barrier, inc=1, device_id=spot, device_id_type=MESH)
        return carry

    lax.fori_loop(1, devices, greet, 0)
    cbuf[pl.ds(me, 1), :, :] = jnp.full((1,) + cbuf.shape[1:], count_ref[0], jnp.int32)

    def count_copy(k, slot):
        other, spot = place(k)
        mine = cbuf.at[pl.ds(me, 1)]
        return pltpu.make_async_remote_copy(
            src_ref=mine,
            dst_ref=cbuf.at[pl.ds(slot(other), 1)],
            send_sem=csend_sem.at[other],
            recv_sem=crecv_sem.at[slot(other)],
            device_id=spot,
            device_id_type=MESH,
        )

    def data_copy(k, slot):
        other, spot = place(k)
        return pltpu.make_async_remote_copy(
            src_ref=send.at[other, pl.ds(0, sent_rows)],
            dst_ref=recv_ref.at[slot(other), pl.ds(0, sent_rows)],
            send_sem=send_sem.at[other],
            recv_sem=recv_sem.at[slot(other)],
            device_id=spot,
            device_id_type=MESH,
        )

    def start_all(make):
        def body(k, carry):
            make(k, lambda other: me).start()
            return carry

        lax.fori_loop(1, devices, body, 0)

    def wait_recv_all(make):
        def body(k, carry):
            make(k, lambda other: other).wait_recv()
            return carry

        lax.fori_loop(1, devices, body, 0)

    def wait_send_all(make):
        def body(k, carry):
            make(k, lambda other: me).wait_send()
            return carry

        lax.fori_loop(1, devices, body, 0)

    row = lax.broadcasted_iota(jnp.int32, (span, LANES), 0)
    labels = lax.rem(row, levels) * devices + row // levels

    total = None
    for c in range(chunks):
        loads[c].wait()
        x = held[pl.ds(c * chunk, chunk), :]
        high = x.astype(jnp.bfloat16)
        low = (x - high.astype(jnp.float32)).astype(jnp.bfloat16)
        parts = []
        for j in range(chunk // LANES):
            at = c * (chunk // LANES) + j
            hit = jnp.where(index_ref[pl.ds(at, 1), :] == labels, 1.0, 0.0)
            if at == 0:
                tally_ref[...] = hit
            else:
                tally_ref[...] += hit
            parts.append(hit.astype(jnp.bfloat16))
        hits = jnp.concatenate(parts, axis=1)
        dot = functools.partial(jnp.dot, preferred_element_type=jnp.float32)
        part = dot(hits, high) + dot(hits, low)
        for h in range(halves):
            block = part[:, h * LANES : (h + 1) * LANES].reshape(devices, levels, LANES)
            if c == 0:
                stage[:, h * levels : (h + 1) * levels, :] = block
            else:
                stage[:, h * levels : (h + 1) * levels, :] += block
        if c == 0:
            pl.semaphore_wait(barrier, devices - 1)
            start_all(count_copy)

    tallies = lax.dot_general(
        jnp.ones((8, LANES), jnp.bfloat16),
        tally_ref[...].astype(jnp.bfloat16),
        (((1,), (1,)), ((), ())),
        preferred_element_type=jnp.float32,
    )[0:1]
    keys = keys_ref[...]
    source = lax.broadcasted_iota(jnp.int32, (span, span), 0)
    goal = lax.broadcasted_iota(jnp.int32, (span, span), 1)
    moved = (source == lax.rem(goal, levels) * devices + goal // levels)
    moved = jnp.where(moved, 1.0, 0.0).astype(jnp.bfloat16)
    line = lax.broadcasted_iota(jnp.int32, (8, span), 0)
    pieces = jnp.where(
        line == 0, keys & 255, jnp.where(line == 1, (keys >> 8) & 255, (keys >> 16) & 255)
    )
    pieces = jnp.dot(
        pieces.astype(jnp.float32).astype(jnp.bfloat16), moved, preferred_element_type=jnp.float32
    )
    placed = pieces[0:1] + pieces[1:2] * 256.0 + pieces[2:3] * 65536.0
    fields = jnp.concatenate([tallies, placed], axis=0)
    for a in range(devices):
        tile = a * levels // LANES * LANES
        stage[a, fields_at : fields_at + 2, :] = fields[:, tile : tile + LANES]

    wait_recv_all(count_copy)
    counts = cbuf[...][:, 0, :]
    sender = lax.broadcasted_iota(jnp.int32, counts.shape, 0)
    lane = lax.broadcasted_iota(jnp.int32, counts.shape, 1)
    counts_ref[...] = jnp.sum(jnp.where(sender == lane, counts, 0), axis=0, keepdims=True)
    before = jnp.sum(jnp.where(sender < me, counts, 0), axis=0, keepdims=True)[0, 0]
    shift = lax.rem(before, devices)

    def roll(k, carry):
        other = lax.rem(me + k, devices)
        send[other] = stage[lax.rem(other - shift + devices, devices)]
        return carry

    lax.fori_loop(1, devices, roll, 0)
    recv_ref[me] = stage[lax.rem(me - shift + devices, devices)]
    start_all(data_copy)
    wait_send_all(count_copy)
    wait_recv_all(data_copy)
    wait_send_all(data_copy)


def place_kernel(
    shape, counts_ref, recv_ref, sums_ref, rows_ref, keys_ref, total_ref, buf
):
    devices, ny, nz, span, levels, fields_at = shape
    me = (lax.axis_index("gx") * ny + lax.axis_index("gy")) * nz + lax.axis_index("gz")
    halves = sums_ref.shape[1] // LANES
    lane = lax.broadcasted_iota(jnp.int32, (8, span), 1)
    fields = jnp.zeros((8, span), jnp.float32)
    offset = jnp.int32(0)

    def step(d, carry):
        offset, fields = carry
        count = counts_ref[0, d]
        first = lax.rem(me - lax.rem(offset, devices) + devices, devices)
        start = (offset + first) // devices
        for h in range(halves):
            buf[h, pl.ds(start, levels), :] = recv_ref[d, h * levels : (h + 1) * levels, :]
        base = lax.rem(first * levels, LANES)
        turn = lax.rem(lax.rem(start, LANES) - base + LANES, LANES)
        tile = recv_ref[d, fields_at : fields_at + 8, :]
        turned = pltpu.roll(tile, turn, 1)
        wide = jnp.concatenate([turned] * (span // LANES), axis=1)
        fields = jnp.where(lane >= start, wide, fields)
        return offset + count, fields

    offset, fields = lax.fori_loop(0, devices, step, (offset, fields), unroll=4)
    total_ref[0, 0] = offset
    taken = (offset - me + devices - 1) // devices
    row = lax.broadcasted_iota(jnp.int32, (span, LANES), 0)
    for h in range(halves):
        sums_ref[:, h * LANES : (h + 1) * LANES] = jnp.where(row < taken, buf[h, 0:span, :], 0.0)
    inside = lane[0:1] < taken
    rows_ref[...] = jnp.where(inside, fields[0:1].astype(jnp.int32), 0)
    keys_ref[...] = jnp.where(inside, fields[1:2].astype(jnp.int32), -1)


def shards(measures, group_index, distinct_keys, group_counts):
    rows, width = measures.shape
    span = distinct_keys.shape[1]
    ny, nz = lax.axis_size("gy"), lax.axis_size("gz")
    devices = lax.axis_size("gx") * ny * nz
    levels = span // devices
    chunks = 4 if rows % (4 * LANES) == 0 else 1
    fields_at = round_up(levels * (width // LANES), 8)
    slab = fields_at + 8
    wide = round_up(devices, LANES)
    vmem = pl.BlockSpec(memory_space=pltpu.VMEM)
    smem = pl.BlockSpec(memory_space=pltpu.SMEM)
    anywhere = pl.BlockSpec(memory_space=pl.ANY)
    received, counts = pl.pallas_call(
        functools.partial(
            exchange_kernel, (devices, ny, nz, span, levels, chunks, fields_at)
        ),
        out_shape=(
            jax.ShapeDtypeStruct((devices, slab, LANES), jnp.float32),
            jax.ShapeDtypeStruct((1, wide), jnp.int32),
        ),
        in_specs=[vmem, vmem, smem, anywhere],
        out_specs=(vmem, vmem),
        scratch_shapes=[
            pltpu.VMEM((rows, width), jnp.float32),
            pltpu.VMEM((devices, slab, LANES), jnp.float32),
            pltpu.VMEM((devices, slab, LANES), jnp.float32),
            pltpu.VMEM((span, LANES), jnp.float32),
            pltpu.VMEM((devices, 1, wide), jnp.int32),
            pltpu.SemaphoreType.DMA((chunks,)),
            pltpu.SemaphoreType.DMA((devices,)),
            pltpu.SemaphoreType.DMA((devices,)),
            pltpu.SemaphoreType.DMA((devices,)),
            pltpu.SemaphoreType.DMA((devices,)),
        ],
        compiler_params=pltpu.CompilerParams(collective_id=0, has_side_effects=True),
        name="exchange",
    )(group_index.reshape(rows // LANES, LANES), distinct_keys, group_counts, measures)
    sums, tallies, keys, total = pl.pallas_call(
        functools.partial(place_kernel, (devices, ny, nz, span, levels, fields_at)),
        out_shape=(
            jax.ShapeDtypeStruct((span, width), jnp.float32),
            jax.ShapeDtypeStruct((1, span), jnp.int32),
            jax.ShapeDtypeStruct((1, span), jnp.int32),
            jax.ShapeDtypeStruct((1, 1), jnp.int32),
        ),
        in_specs=[smem, vmem],
        out_specs=(vmem, vmem, vmem, smem),
        scratch_shapes=[pltpu.VMEM((width // LANES, span + round_up(levels, 8), LANES), jnp.float32)],
        name="place",
    )(counts, received)
    return sums, tallies.reshape(span), keys.reshape(span), total.reshape(())


def solution(mesh):
    return jax.shard_map(
        shards,
        mesh=mesh,
        in_specs=(
            P(AXES, None),
            P(AXES),
            P(AXES, None),
            P(AXES),
        ),
        out_specs=(P(AXES, None), P(AXES), P(AXES), P()),
        check_vma=False,
    )
```

time: 107 us -> 32.6 us (0.30)
  blocking collectives: 42 us -> 0 us
  Pallas kernels: 0 us -> 31 us
  waiting for transfers between devices: 20.1 us -> 0 us
  local copies, waits for them, and re-layouts: 17.5 us -> 0 us
  starting transfers between devices: 14.1 us -> 0 us
  matrix products: 5.34 us -> 0 us
  other arithmetic: 3.86 us -> 0 us
  between operations: 3.41 us -> 1.29 us
    unnamed x1 -> x0, blocking collectives: 42 us -> none
    pallas_call x0 -> x2, Pallas kernels: none -> 31 us  [the longest x1 28.3 us: shards(): pl.pallas_call(functools.partial(exchange_kernel, (devices, ny, nz, span,...]
    all_to_all x4 -> x0, waiting for transfers between devices: 20.1 us -> none  [the longest x1 10.3 us: shards(): lax.all_to_all(outgoing[0], 'gz', split_axis=2, concat_axis=2, tiled=True)]
    all_to_all x4 -> x0, starting transfers between devices: 14.1 us -> none  [the longest x1 3.6 us: shards(): lax.all_to_all(outgoing[1], 'gz', split_axis=2, concat_axis=2, tiled=True)]
    scatter x3 -> x0, local copies, waits for them, and re-layouts: 9.01 us -> none  [the longest x1 3.02 us: shards(): group_sums = jnp.zeros((span, width), jnp.float32).at[target].set(got_sum...]
    dot_general x2 -> x0, matrix products: 5.34 us -> none  [accumulate(): jnp.dot(hits.astype(jnp.float32), values, precision=lax.Precision.HIGHEST...]
    dynamic_slice x5 -> x0, local copies, waits for them, and re-layouts: 2.35 us -> none  [the longest x2 1.39 us: accumulate(): index = lax.dynamic_slice_in_dim(group_index, start, block)]
    unnamed x9 -> x0, local copies, waits for them, and re-layouts: 2.18 us -> none
  transfers between devices with their start and end apart: 4 -> 0, of which waited for: 4 -> 0; matrix products, arithmetic and copies ran while one was open for 12% -> 0% of each run, Pallas kernels for 0% -> 0%
where the time goes in v1:
time: 32.6 us; the launch traced here: 32.3 us
  Pallas kernels  31 us (95%)
  between operations  1.29 us (4%)
    pallas_call x1, Pallas kernels, shards(): pl.pallas_call(functools.partial(exchange_kernel, (devices, ny, nz, span,...  28.3 us
    pallas_call x1, Pallas kernels, shards(): pl.pallas_call(functools.partial(place_kernel, (devices, ny, nz, span, le...  2.78 us

profile of v1, /device:TPU:0, one launch (start us, length us, event | category | flops | bytes accessed | tf_op | source)
XLA Modules:
  0.0 32.3 jit_solution(16224817122654841953)
XLA Ops:
  1.3 28.3 %exchange.1 = (f32[32,40,128]{2,1,0:T(8,128)}, s32[1,128]{1,0:T(1,128)}) custom-call(s32[16,128]{1,0:T(8,128)} %bitcast.4, s32[1,512]{1,0:T(1,128)} %keys_ref.1, s32[1]{0:T(128)S(6)} %copy.8.count_ref, f32[2048,256]{1,0:T(8,128)} %measures_ref.1), custom_call_target="tpu_custom_call" | custom-call | tf_op jit(solution)/shard_map/exchange/pallas_call | solution.py:235
  29.5 2.8 %place.1 = (f32[512,256]{1,0:T(8,128)}, s32[1,512]{1,0:T(1,128)}, s32[1,512]{1,0:T(1,128)}, s32[1,1]{1,0:T(1,128)}) custom-call(s32[1,128]{1,0:T(1,128)} %get-tuple-element.10.counts_ref, f32[32,40,128]{2,1,0:T(8,128)} %get-tuple-element.11.recv_ref), custom_call_target="tpu_custom_call" | custom-call | tf_op jit(solution)/shard_map/place/pallas_call | solution.py:260

commit v2 on v1

v2 whole, which is shorter than its diff:
```python
import functools

import jax
import jax.numpy as jnp
from jax import lax
from jax.experimental import pallas as pl
from jax.experimental.pallas import tpu as pltpu
from jax.sharding import PartitionSpec as P

AXES = ("gx", "gy", "gz")
LANES = 128
MESH = pl.DeviceIdType.MESH


def round_up(value, unit):
    return (value + unit - 1) // unit * unit


def steps_of(dims):
    nx, ny, nz = dims
    far = [(a, b, c) for c in range(nz) for a in range(nx) for b in range(ny)]
    far.sort(key=lambda k: -min(k[2], nz - k[2]))
    return [((a * ny + b) * nz + c, (a, b, c)) for a, b, c in far if (a, b, c) != (0, 0, 0)]


def wrapped(value, size):
    return jnp.where(value >= size, value - size, value)


def modulo(value, size):
    if size & (size - 1) == 0:
        return value & (size - 1)
    return lax.rem(value, size)


def divide(value, size):
    if size & (size - 1) == 0:
        return lax.shift_right_arithmetic(value, jnp.int32(size.bit_length() - 1))
    return value // size


def exchange_kernel(
    shape,
    index_hbm,
    keys_hbm,
    count_hbm,
    measures_ref,
    recv_ref,
    counts_ref,
    held,
    stage,
    send,
    tally_ref,
    cbuf,
    index_ref,
    keys_ref,
    count_ref,
    small_sem,
    load_sem,
    count_sem,
    data_sem,
):
    dims, span, levels, chunks, fields_at = shape
    nx, ny, nz = dims
    devices = nx * ny * nz
    spots = [lax.axis_index(axis) for axis in AXES]
    me = (spots[0] * ny + spots[1]) * nz + spots[2]
    ring = [[wrapped(spot + k, size) for k in range(size)] for spot, size in zip(spots, dims)]
    rows, width = held.shape
    chunk = rows // chunks
    halves = width // LANES
    sent_rows = fields_at + 2
    steps = steps_of(dims)

    count_load = pltpu.make_async_copy(count_hbm, count_ref, small_sem.at[0])
    count_load.start()
    barrier = pltpu.get_barrier_semaphore()
    for _, k in steps:
        pl.semaphore_signal(
            barrier, inc=1, device_id=tuple(r[i] for r, i in zip(ring, k)), device_id_type=MESH
        )
    index_load = pltpu.make_async_copy(index_hbm, index_ref, small_sem.at[1])
    index_load.start()
    loads = []
    for c in range(chunks):
        piece = pl.ds(c * chunk, chunk)
        load = pltpu.make_async_copy(measures_ref.at[piece], held.at[piece], load_sem.at[c])
        load.start()
        loads.append(load)
    keys_load = pltpu.make_async_copy(keys_hbm, keys_ref, small_sem.at[2])
    keys_load.start()

    def remote(source, goal, sems, k):
        return pltpu.make_async_remote_copy(
            src_ref=source,
            dst_ref=goal,
            send_sem=sems.at[0],
            recv_sem=sems.at[1],
            device_id=tuple(r[i] for r, i in zip(ring, k)),
            device_id_type=MESH,
        )

    count_load.wait()
    cbuf[0] = jnp.broadcast_to(count_ref[...], cbuf.shape[1:])
    index_load.wait()

    row = lax.broadcasted_iota(jnp.int32, (span, LANES), 0)
    labels = lax.rem(row, levels) * devices + row // levels

    total = None
    for c in range(chunks):
        loads[c].wait()
        x = held[pl.ds(c * chunk, chunk), :]
        high = x.astype(jnp.bfloat16)
        low = (x - high.astype(jnp.float32)).astype(jnp.bfloat16)
        parts = []
        for j in range(chunk // LANES):
            at = c * (chunk // LANES) + j
            hit = jnp.where(index_ref[pl.ds(at, 1), :] == labels, 1.0, 0.0)
            if at == 0:
                tally_ref[...] = hit
            else:
                tally_ref[...] += hit
            parts.append(hit.astype(jnp.bfloat16))
        hits = jnp.concatenate(parts, axis=1)
        dot = functools.partial(jnp.dot, preferred_element_type=jnp.float32)
        part = dot(hits, high) + dot(hits, low)
        for h in range(halves):
            block = part[:, h * LANES : (h + 1) * LANES].reshape(devices, levels, LANES)
            if c == 0:
                stage[:, h * levels : (h + 1) * levels, :] = block
            else:
                stage[:, h * levels : (h + 1) * levels, :] += block
        if c == 0:
            pl.semaphore_wait(barrier, devices - 1)
            for slot, k in steps:
                remote(cbuf.at[0], cbuf.at[slot], count_sem, k).start()

    tallies = lax.dot_general(
        jnp.ones((8, LANES), jnp.bfloat16),
        tally_ref[...].astype(jnp.bfloat16),
        (((1,), (1,)), ((), ())),
        preferred_element_type=jnp.float32,
    )[0:1]
    keys_load.wait()
    keys = keys_ref[...]
    source = lax.broadcasted_iota(jnp.int32, (span, span), 0)
    goal = lax.broadcasted_iota(jnp.int32, (span, span), 1)
    moved = (source == lax.rem(goal, levels) * devices + goal // levels)
    moved = jnp.where(moved, 1.0, 0.0).astype(jnp.bfloat16)
    line = lax.broadcasted_iota(jnp.int32, (8, span), 0)
    pieces = jnp.where(
        line == 0, keys & 255, jnp.where(line == 1, (keys >> 8) & 255, (keys >> 16) & 255)
    )
    pieces = jnp.dot(
        pieces.astype(jnp.float32).astype(jnp.bfloat16), moved, preferred_element_type=jnp.float32
    )
    placed = pieces[0:1] + pieces[1:2] * 256.0 + pieces[2:3] * 65536.0
    fields = jnp.concatenate([tallies, placed], axis=0)
    for a in range(devices):
        tile = a * levels // LANES * LANES
        stage[a, fields_at : fields_at + 2, :] = fields[:, tile : tile + LANES]

    others = cbuf.at[pl.ds(1, devices - 1)]
    pltpu.make_async_copy(others, others, count_sem.at[1]).wait()
    counts = cbuf[...][:, 0, :]
    slots = lax.broadcasted_iota(jnp.int32, counts.shape, 0)
    parts = (divide(slots, ny * nz), modulo(divide(slots, nz), ny), modulo(slots, nz))
    back = [
        jnp.where(spot >= part, spot - part, spot - part + size)
        for spot, part, size in zip(spots, parts, dims)
    ]
    sender = (back[0] * ny + back[1]) * nz + back[2]
    lane = lax.broadcasted_iota(jnp.int32, counts.shape, 1)
    counts_ref[...] = jnp.sum(jnp.where(sender == lane, counts, 0), axis=0, keepdims=True)
    before = jnp.sum(jnp.where(sender < me, counts, 0), axis=0, keepdims=True)[0, 0]
    shift = modulo(before, devices)

    for slot, (a, b, c) in steps:
        other = (ring[0][a] * ny + ring[1][b]) * nz + ring[2][c]
        send[slot] = stage[modulo(other - shift + devices, devices)]
    for slot, k in steps:
        piece = pl.ds(0, sent_rows)
        remote(send.at[slot, piece], recv_ref.at[slot, piece], data_sem, k).start()
    recv_ref[0] = stage[modulo(me - shift + devices, devices)]
    pltpu.make_async_copy(others, others, count_sem.at[0]).wait()
    landed = recv_ref.at[pl.ds(1, devices - 1), pl.ds(0, sent_rows)]
    left = send.at[pl.ds(1, devices - 1), pl.ds(0, sent_rows)]
    pltpu.make_async_copy(left, left, data_sem.at[0]).wait()
    pltpu.make_async_copy(landed, landed, data_sem.at[1]).wait()


def place_kernel(
    shape, counts_ref, recv_ref, sums_ref, rows_ref, keys_ref, total_ref, buf
):
    dims, span, levels, fields_at = shape
    nx, ny, nz = dims
    devices = nx * ny * nz
    spots = [lax.axis_index(axis) for axis in AXES]
    me = (spots[0] * ny + spots[1]) * nz + spots[2]
    back = [
        [jnp.where(spot >= k, spot - k, spot - k + size) for k in range(size)]
        for spot, size in zip(spots, dims)
    ]
    halves = sums_ref.shape[1] // LANES
    lane = lax.broadcasted_iota(jnp.int32, (8, span), 1)
    fields = jnp.zeros((8, span), jnp.float32)
    offset = jnp.int32(0)

    for d in range(devices):
        slot = (back[0][d // (ny * nz)] * ny + back[1][d // nz % ny]) * nz + back[2][d % nz]
        first = modulo(me - modulo(offset, devices) + devices, devices)
        start = divide(offset + first, devices)
        for h in range(halves):
            buf[h, pl.ds(start, levels), :] = recv_ref[slot, h * levels : (h + 1) * levels, :]
        turn = modulo(modulo(start, LANES) - modulo(first * levels, LANES) + LANES, LANES)
        turned = pltpu.roll(recv_ref[slot, fields_at : fields_at + 8, :], turn, 1)
        wide = jnp.concatenate([turned] * (span // LANES), axis=1)
        fields = jnp.where(lane >= start, wide, fields)
        offset = offset + counts_ref[0, d]

    total_ref[0, 0] = offset
    taken = divide(offset - me + devices - 1, devices)
    row = lax.broadcasted_iota(jnp.int32, (span, LANES), 0)
    for h in range(halves):
        sums_ref[:, h * LANES : (h + 1) * LANES] = jnp.where(row < taken, buf[h, 0:span, :], 0.0)
    inside = lane[0:1] < taken
    rows_ref[...] = jnp.where(inside, fields[0:1].astype(jnp.int32), 0)
    keys_ref[...] = jnp.where(inside, fields[1:2].astype(jnp.int32), -1)


def shards(measures, group_index, distinct_keys, group_counts):
    rows, width = measures.shape
    span = distinct_keys.shape[1]
    dims = tuple(lax.axis_size(axis) for axis in AXES)
    devices = dims[0] * dims[1] * dims[2]
    levels = span // devices
    chunks = 4 if rows % (4 * LANES) == 0 else 1
    fields_at = round_up(levels * (width // LANES), 8)
    slab = fields_at + 8
    wide = round_up(devices, LANES)
    vmem = pl.BlockSpec(memory_space=pltpu.VMEM)
    smem = pl.BlockSpec(memory_space=pltpu.SMEM)
    anywhere = pl.BlockSpec(memory_space=pl.ANY)
    received, counts = pl.pallas_call(
        functools.partial(
            exchange_kernel, (dims, span, levels, chunks, fields_at)
        ),
        out_shape=(
            jax.ShapeDtypeStruct((devices, slab, LANES), jnp.float32),
            jax.ShapeDtypeStruct((1, wide), jnp.int32),
        ),
        in_specs=[anywhere] * 4,
        out_specs=(vmem, vmem),
        scratch_shapes=[
            pltpu.VMEM((rows, width), jnp.float32),
            pltpu.VMEM((devices, slab, LANES), jnp.float32),
            pltpu.VMEM((devices, slab, LANES), jnp.float32),
            pltpu.VMEM((span, LANES), jnp.float32),
            pltpu.VMEM((devices, 1, wide), jnp.int32),
            pltpu.VMEM((rows // LANES, LANES), jnp.int32),
            pltpu.VMEM((1, span), jnp.int32),
            pltpu.VMEM((1, 1), jnp.int32),
            pltpu.SemaphoreType.DMA((3,)),
            pltpu.SemaphoreType.DMA((chunks,)),
            pltpu.SemaphoreType.DMA((2,)),
            pltpu.SemaphoreType.DMA((2,)),
        ],
        compiler_params=pltpu.CompilerParams(collective_id=0, has_side_effects=True),
        name="exchange",
    )(group_index.reshape(rows // LANES, LANES), distinct_keys, group_counts.reshape(1, 1), measures)
    sums, tallies, keys, total = pl.pallas_call(
        functools.partial(place_kernel, (dims, span, levels, fields_at)),
        out_shape=(
            jax.ShapeDtypeStruct((span, width), jnp.float32),
            jax.ShapeDtypeStruct((1, span), jnp.int32),
            jax.ShapeDtypeStruct((1, span), jnp.int32),
            jax.ShapeDtypeStruct((1, 1), jnp.int32),
        ),
        in_specs=[smem, vmem],
        out_specs=(vmem, vmem, vmem, smem),
        scratch_shapes=[pltpu.VMEM((width // LANES, span + round_up(levels, 8), LANES), jnp.float32)],
        name="place",
    )(counts, received)
    return sums, tallies.reshape(span), keys.reshape(span), total.reshape(())


def solution(mesh):
    return jax.shard_map(
        shards,
        mesh=mesh,
        in_specs=(
            P(AXES, None),
            P(AXES),
            P(AXES, None),
            P(AXES),
        ),
        out_specs=(P(AXES, None), P(AXES), P(AXES), P()),
        check_vma=False,
    )
```

time: 32.6 us -> 27.5 us (0.84)
  Pallas kernels: 31 us -> 25.9 us
    pallas_call x2, Pallas kernels: 31 us -> 25.9 us  [the longest x1 23.7 us: shards(): pl.pallas_call(functools.partial(exchange_kernel, (dims, span, levels, ch...]
where the time goes in v2:
time: 27.5 us; the launch traced here: 27.2 us
  Pallas kernels  25.9 us (94%)
  between operations  1.29 us (5%)
    pallas_call x1, Pallas kernels, shards(): pl.pallas_call(functools.partial(exchange_kernel, (dims, span, levels, ch...  23.7 us
    pallas_call x1, Pallas kernels, shards(): pl.pallas_call(functools.partial(place_kernel, (dims, span, levels, field...  2.18 us

profile of v2, /device:TPU:0, one launch (start us, length us, event | category | flops | bytes accessed | tf_op | source)
XLA Modules:
  0.0 27.2 jit_solution(4739961040846989106)
XLA Ops:
  1.3 23.7 %exchange.1 = (f32[32,40,128]{2,1,0:T(8,128)}, s32[1,128]{1,0:T(1,128)}) custom-call(s32[16,128]{1,0:T(8,128)} %bitcast.6, s32[1,512]{1,0:T(1,128)} %keys_hbm.1, s32[1,1]{1,0:T(1,128)} %bitcast.5.count_hbm, f32[2048,256]{1,0:T(8,128)} %measures_ref.1), custom_call_target="tpu_custom_call" | custom-call | tf_op jit(solution)/shard_map/exchange/pallas_call | solution.py:245
  25.0 2.2 %place.1 = (f32[512,256]{1,0:T(8,128)}, s32[1,512]{1,0:T(1,128)}, s32[1,512]{1,0:T(1,128)}, s32[1,1]{1,0:T(1,128)}) custom-call(s32[1,128]{1,0:T(1,128)} %get-tuple-element.10.counts_ref, f32[32,40,128]{2,1,0:T(8,128)} %get-tuple-element.11.recv_ref), custom_call_target="tpu_custom_call" | custom-call | tf_op jit(solution)/shard_map/place/pallas_call | solution.py:272

commit v3 on v2

--- a/solution.py
+++ b/solution.py
@@ -247,8 +247,8 @@
             exchange_kernel, (dims, span, levels, chunks, fields_at)
         ),
         out_shape=(
-            jax.ShapeDtypeStruct((devices, slab, LANES), jnp.float32),
-            jax.ShapeDtypeStruct((1, wide), jnp.int32),
+            pltpu.VMEM((devices, slab, LANES), jnp.float32),
+            pltpu.VMEM((1, wide), jnp.int32),
         ),
         in_specs=[anywhere] * 4,
         out_specs=(vmem, vmem),
@@ -280,8 +280,9 @@
         in_specs=[smem, vmem],
         out_specs=(vmem, vmem, vmem, smem),
         scratch_shapes=[pltpu.VMEM((width // LANES, span + round_up(levels, 8), LANES), jnp.float32)],
+        compiler_params=pltpu.CompilerParams(vmem_limit_bytes=16 * 1024 * 1024),
         name="place",
-    )(counts, received)
+    )(*(pltpu.with_memory_space_constraint(part, pltpu.VMEM) for part in (counts, received)))
     return sums, tallies.reshape(span), keys.reshape(span), total.reshape(())
 
 

time: 27.5 us -> 26.1 us (0.949)
  Pallas kernels: 25.9 us -> 24.5 us
    pallas_call x1, Pallas kernels: 23.7 us -> 22.9 us  [shards(): pl.pallas_call(functools.partial(exchange_kernel, (dims, span, levels, ch...]
    pallas_call x1, Pallas kernels: 2.18 us -> 1.63 us  [shards(): pl.pallas_call(functools.partial(place_kernel, (dims, span, levels, field...]
where the time goes in v3:
time: 26.1 us; the launch traced here: 25.8 us
  Pallas kernels  24.5 us (94%)
  between operations  1.29 us (5%)
    pallas_call x1, Pallas kernels, shards(): pl.pallas_call(functools.partial(exchange_kernel, (dims, span, levels, ch...  22.9 us
    pallas_call x1, Pallas kernels, shards(): pl.pallas_call(functools.partial(place_kernel, (dims, span, levels, field...  1.63 us

profile of v3, /device:TPU:0, one launch (start us, length us, event | category | flops | bytes accessed | tf_op | source)
XLA Modules:
  0.0 25.8 jit_solution(12453018492436540009)
XLA Ops:
  1.3 22.9 %exchange.1 = (f32[32,40,128]{2,1,0:T(8,128)S(1)}, s32[1,128]{1,0:T(1,128)S(1)}) custom-call(s32[16,128]{1,0:T(8,128)} %bitcast.6, s32[1,512]{1,0:T(1,128)} %keys_hbm.1, s32[1,1]{1,0:T(1,128)} %bitcast.5.count_hbm, f32[2048,256]{1,0:T(8,128)} %measures_ref.1), custom_call_target="tpu_custom_call" | custom-call | tf_op jit(solution)/shard_map/exchange/pallas_call | solution.py:245
  24.2 1.6 %place.1 = (f32[512,256]{1,0:T(8,128)}, s32[1,512]{1,0:T(1,128)}, s32[1,512]{1,0:T(1,128)}, s32[1,1]{1,0:T(1,128)}) custom-call(s32[1,128]{1,0:T(1,128)S(1)} %get-tuple-element.10.counts_ref, f32[32,40,128]{2,1,0:T(8,128)S(1)} %get-tuple-element.11.recv_ref), custom_call_target="tpu_custom_call" | custom-call | tf_op jit(solution)/shard_map/place/pallas_call | solution.py:272
